TPU v7x, 256 devices: a 4x2x16 block of a 4x16x16 slice. The times are simulated.
256 devices in a mesh: site: 2 (over y), pts: 128 (over z, x, core).
Axes of the slice: x: 4, y: 2, z: 16, core: 2. Of those that a mesh axis runs over, the one named last changes fastest.
The devices are a block of a 4x16x16 slice.
Arguments:
- green_tensors: bfloat16 [4096, 4, 6, 2, 1024], P(('site', 'pts')), parts along dimension 0, may hold values from -6 to 6
- block_lists: int32 [256, 32], P(('site', 'pts')), parts along dimension 0, may hold values from 0 to 2047, as said below
- block_count: int32 [256], P(('site', 'pts')), parts along dimension 0, may hold values from 1 to 32
- onset_steps: int32 [256, 16, 128], P(('site', 'pts')), parts along dimension 0, may hold values from 0 to 255
- slip_amount: float32 [256, 16, 128], P(('site', 'pts')), parts along dimension 0, may hold values from 0.2 to 2
- mechanism: float32 [256, 6], P(('site', 'pts')), parts along dimension 0, may hold values from -2.4 to 2.4
- slip_rate: float32 [256, 16, 128], P(('site', 'pts')), parts along dimension 0, may hold values from 0.005 to 0.05
Outputs:
- seismograms: float32 [256, 16, 2, 1024], P(('site', 'pts')), parts along dimension 0
There are 2 independent parts, one for each index of `site`. A program takes and returns all parts, laid end to end along the dimension named above; each array names one. Nothing has to cross between parts.
Inputs may be any that keep to these rules, and one draw needn't show every extreme that they name: `block_lists`: numbers of point blocks; the ruptures held by one device name at most 1 entries in blocks held by any one device, and exactly 1 for some holder.
All inputs are finite; a program needn't handle non-finite values.
Results may differ from a plain program's by a relative error of at most 0.0003.
Values may be sent and summed in bfloat16 or wider, within the bound.
A program may use at most 128 MiB of HBM per device.

v0:
```python
import jax
import jax.numpy as jnp
from jax import lax
from jax.sharding import Mesh
from jax.sharding import PartitionSpec as P

MAXON = 256
PTS = ("pts_0", "pts_1", "pts_2")
SITE_PTS = ("site", "pts_0", "pts_1", "pts_2")


def laid_out(blocks, dim):
    blocks = jnp.moveaxis(blocks, 0, dim)
    lengths = blocks.shape
    return blocks.reshape(*lengths[:dim], lengths[dim] * lengths[dim + 1], *lengths[dim + 2 :])


def stacked_from(value, axes, turns):
    blocks = value[None]
    for k in turns:
        blocks = lax.all_gather(blocks, axes[k], axis=0, tiled=True)
    held = [lax.axis_size(axes[k]) for k in reversed(turns)]
    blocks = blocks.reshape(*held, *value.shape)
    turned = sorted(range(len(turns)), key=lambda place: turns[len(turns) - 1 - place])
    return blocks.transpose(*turned, *range(len(turns), blocks.ndim)).reshape(-1, *value.shape)


def gather_axes(value, axes, turns, dim):
    return laid_out(stacked_from(value, axes, turns), dim)


def lag_traces(traces, onsets):
    length = traces.shape[-1]
    shifted_all = traces
    for bit_index in range((MAXON - 1).bit_length()):
        stride = 1 << bit_index
        shifted = jnp.pad(shifted_all, ((0, 0), (0, 0), (stride, 0)))[:, :, :length]
        bit_set = jnp.bitwise_and(jnp.right_shift(onsets, bit_index), 1) == 1
        shifted_all = jnp.where(bit_set[:, None, None], shifted, shifted_all)
    return shifted_all


def weighted_sum(traces, weights, onsets):

    def per_variation(weight_row, onset_row):
        return jnp.sum(weight_row[:, None, None] * lag_traces(traces, onset_row), axis=0)

    return jax.vmap(per_variation)(weights, onsets)


def convolve_rate(motion, slip_rate):
    taps = slip_rate.shape[-1]
    length = motion.shape[-1]
    offset = jnp.arange(taps, dtype=jnp.int32)[None, :] - jnp.arange(taps, dtype=jnp.int32)[:, None]
    near = jnp.where(offset >= 0, jnp.take(slip_rate, jnp.clip(offset, 0, taps - 1), axis=-1), 0.0)
    far = jnp.where(
        offset < 0, jnp.take(slip_rate, jnp.clip(offset + taps, 0, taps - 1), axis=-1), 0.0
    )
    blocked = motion.reshape(motion.shape[:-1] + (length // taps, taps))
    earlier = jnp.pad(blocked, ((0, 0), (0, 0), (0, 0), (1, 0), (0, 0)))[:, :, :, :-1, :]
    result = jnp.einsum("rvcbi,rvij->rvcbj", blocked, near, precision=lax.Precision.HIGHEST)
    result = result + jnp.einsum("rvcbi,rvij->rvcbj", earlier, far, precision=lax.Precision.HIGHEST)
    return result.reshape(motion.shape)


def local(green_tensors, block_lists, block_count, onset_steps, slip_amount, mechanism, slip_rate):
    held = green_tensors.shape[0]
    points = green_tensors.shape[1]
    length = green_tensors.shape[-1]
    ruptures, listed = block_lists.shape
    devices = lax.axis_size(PTS)
    capacity = max(1, ruptures * listed // devices)
    own_index = lax.axis_index(PTS)
    entries = ruptures * listed
    every_list = gather_axes(block_lists, PTS, (0, 1, 2), 0)
    holder = every_list // held
    local_block = every_list % held
    order = jnp.arange(entries, dtype=jnp.int32)
    earlier_same = (holder[:, :, None] == holder[:, None, :]) & (
        order[None, None, :] < order[None, :, None]
    )
    slot_rank = jnp.sum(earlier_same.astype(jnp.int32), axis=2)
    slot_ids = jnp.arange(capacity, dtype=jnp.int32)
    chosen = (
        (holder == own_index)[:, None, :] & (slot_rank[:, None, :] == slot_ids[None, :, None])
    ).astype(jnp.int32)
    slot_block = jnp.sum(chosen * local_block[:, None, :], axis=2)
    slot_entry = jnp.sum(chosen * order[None, None, :], axis=2)
    worker_ids = jnp.arange(devices, dtype=jnp.int32)[:, None]
    my_holder = block_lists.reshape(entries) // held
    my_rank = lax.dynamic_index_in_dim(slot_rank, own_index, 0, keepdims=False)
    source_row = my_holder * capacity + my_rank
    kept_mask = (jnp.arange(listed, dtype=jnp.int32)[None, :] < block_count[:, None]).astype(
        jnp.float32
    )
    weights = slip_amount * jnp.repeat(kept_mask, points, axis=1)[:, None, :]

    def rupture_motion(inputs):
        rupture_traces, weight_rows, onset_rows = inputs
        return weighted_sum(rupture_traces.reshape(-1, 2, length), weight_rows, onset_rows)

    every_mech = gather_axes(mechanism, PTS, (1, 0, 2), 0).reshape(devices, ruptures, 6)
    slot_mech = every_mech[worker_ids, slot_entry // listed]
    picked = jnp.take(green_tensors, slot_block.reshape(-1), axis=0)
    picked = picked.reshape((devices, capacity) + green_tensors.shape[1:]).astype(jnp.float32)
    outgoing = jnp.einsum("wcpsgt,wcs->wcpgt", picked, slot_mech, precision=lax.Precision.HIGHEST)
    incoming = lax.all_to_all(outgoing, PTS, split_axis=0, concat_axis=0, tiled=True)
    flat_rows = incoming.reshape(devices * capacity, points, 2, length)
    traces = jnp.take(flat_rows, source_row, axis=0).reshape(ruptures, listed, points, 2, length)
    motion = lax.map(rupture_motion, (traces, weights, onset_steps))
    return convolve_rate(motion, slip_rate)


def solution(mesh):
    split = Mesh(
        mesh.devices.reshape(mesh.shape["site"], 16, 4, 2), ("site", "pts_0", "pts_1", "pts_2")
    )
    placed = (
        P(SITE_PTS, None, None, None, None),
        P(SITE_PTS, None),
        P(SITE_PTS),
        P(SITE_PTS, None, None),
        P(SITE_PTS, None, None),
        P(SITE_PTS, None),
        P(SITE_PTS, None, None),
    )
    return jax.shard_map(
        local, mesh=split, in_specs=placed, out_specs=P(SITE_PTS, None, None, None), check_vma=False
    )
```

profile of v0, /device:TPU:35, one launch (start us, length us, event | category | flops | bytes accessed | tf_op | source)
XLA Modules:
  0.0 476.5 jit_solution(1629342258977329631)
XLA Ops:
  0.0 41.4 %all-gather.6 = s32[16,1,32]{2,1,0:T(1,128)S(1)} all-gather(s32[1,1,32]{2,1,0:T(1,128)} %bitcast.137), channel_id=2, replica_groups=mesh['site'=2,'pts_0'=16,'pts_1'=4,'pts_2'=2] {'pts_0'}, dimensions={0}, use_global_device_ids=true | all-gather | bytes 2176 | tf_op jit(solution)/shard_map/all_gather | solution.py:21
  41.4 9.4 %all-gather.1 = s32[64,32]{1,0:T(8,128)S(1)} all-gather(s32[16,32]{1,0:T(8,128)S(1)} %bitcast.134), channel_id=3, replica_groups=mesh['site'=2,'pts_0'=16,'pts_1'=4,'pts_2'=2] {'pts_1'}, dimensions={0}, use_global_device_ids=true | all-gather | bytes 10240 | tf_op jit(solution)/shard_map/all_gather | solution.py:21
  50.9 12.2 %all-gather.7 = s32[2,64,32]{1,2,0:T(8,128)S(1)} all-gather(s32[1,64,32]{1,2,0:T(8,128)S(1)} %copy.84), channel_id=4, replica_groups=mesh['site'=2,'pts_0'=16,'pts_1'=4,'pts_2'=2] {'pts_2'}, dimensions={0}, use_global_device_ids=true | all-gather | bytes 24576 | tf_op jit(solution)/shard_map/all_gather | solution.py:21
  63.8 0.4 fusion.30
  64.9 5.8 %all-gather.8 = f32[4,1,6]{2,1,0:T(1,128)S(1)} all-gather(f32[1,1,6]{2,1,0:T(1,128)} %bitcast.136), channel_id=5, replica_groups=mesh['site'=2,'pts_0'=16,'pts_1'=4,'pts_2'=2] {'pts_1'}, dimensions={0}, use_global_device_ids=true | all-gather | bytes 120 | tf_op jit(solution)/shard_map/all_gather | solution.py:21
  70.7 19.3 %all-gather.9 = f32[16,4,6]{2,1,0:T(4,128)S(1)} all-gather(f32[1,4,6]{2,1,0:T(4,128)S(1)} %bitcast.135), channel_id=6, replica_groups=mesh['site'=2,'pts_0'=16,'pts_1'=4,'pts_2'=2] {'pts_0'}, dimensions={0}, use_global_device_ids=true | all-gather | bytes 1632 | tf_op jit(solution)/shard_map/all_gather | solution.py:21
  90.1 11.1 %all-gather.10 = f32[2,64,6]{1,2,0:T(8,128)S(1)} all-gather(f32[1,64,6]{1,2,0:T(8,128)S(1)} %copy.95), channel_id=7, replica_groups=mesh['site'=2,'pts_0'=16,'pts_1'=4,'pts_2'=2] {'pts_2'}, dimensions={0}, use_global_device_ids=true | all-gather | bytes 4608 | tf_op jit(solution)/shard_map/all_gather | solution.py:21
  101.6 27.6 %gather_fusion = bf16[128,4,6,2,1024]{4,3,2,1,0:T(2,128)(2,1)} fusion(bf16[16,4,6,2,1024]{4,3,2,1,0:T(2,128)(2,1)S(1)} %copy-done, s32[1024]{0:T(1024)S(1)} %pad_clamp_fusion.1), kind=kCustom, calls=%fused_computation.2 | custom fusion | bytes 25166336 | tf_op jit(solution)/shard_map/jit(_take)/gather | solution.py:104
  129.3 15.3 %broadcast_select_fusion = bf16[128,4,6,2,1024]{4,3,2,1,0:T(2,128)(2,1)} fusion(bf16[128,4,6,2,1024]{4,3,2,1,0:T(2,128)(2,1)} %gather_fusion, pred[128]{0:T(512)(128)(4,1)S(1)} %compare_and_fusion), kind=kLoop, calls=%fused_computation.5 | loop fusion | flops 6291456 | bytes 25165952 | tf_op jit(solution)/shard_map/jit(_take)/select_n | solution.py:104
  144.6 0.7 gather_fusion.1
  145.3 29.9 %fusion.9 = f32[128,1,4,2,1024]{4,1,3,2,0:T(1,128)S(1)} fusion(f32[128,6,1,1,1]{1,2,4,3,0:T(1,128)S(1)} %bitcast.133, bf16[128,4,6,2,1024]{4,3,2,1,0:T(2,128)(2,1)} %broadcast_select_fusion), kind=kOutput, calls=%fused_computation.22 | convolution fusion | flops 75497472 | bytes 16780288 | tf_op jit(solution)/shard_map/wcpsgt,wcs->wcpgt/dot_general | solution.py:106
  175.2 4.1 copy.114
  179.3 10.4 %all-to-all-start = ((f32[128,1,4,2,1024]{4,3,2,1,0:T(2,128)}), f32[128,1,4,2,1024]{4,3,2,1,0:T(2,128)}, u32[]{:S(2)}, u32[]{:S(2)}) async-start(f32[128,1,4,2,1024]{4,3,2,1,0:T(2,128)} %bitcast.123), calls=%async_computation | async-start | bytes 8388608 | tf_op jit(solution)/shard_map/all_to_all | solution.py:107
  191.1 54.4 %gather_fusion.3 = f32[16384,16]{1,0:T(8,128)} fusion(f32[16,128]{0,1:T(8,128)S(1)} %bitcast.121, s32[16384]{0:T(1024)S(1)} %bitcast_clamp_fusion.1), kind=kCustom, calls=%fused_computation.clone | custom fusion | bytes 2162688 | tf_op jit(solution)/shard_map/jit(_take)/gather | solution.py:55
  245.6 5.2 %copy.102 = f32[128,128,16]{1,0,2:T(8,128)S(1)} copy(f32[128,128,16]{2,1,0:T(8,128)} %bitcast.125) | data formatting | bytes 2097152 | tf_op jit(solution)/shard_map/jit(_take)/gather | solution.py:55
  250.8 54.4 %gather_fusion.4 = f32[16384,16]{1,0:T(8,128)} fusion(f32[16,128]{0,1:T(8,128)S(1)} %bitcast.122, s32[16384]{0:T(1024)S(1)} %bitcast_clamp_fusion), kind=kCustom, calls=%fused_computation.1.clone | custom fusion | bytes 2162688 | tf_op jit(solution)/shard_map/jit(_take)/gather | solution.py:57
  305.2 6.1 %copy.104 = f32[128,128,16]{1,0,2:T(8,128)} copy(f32[128,128,16]{2,1,0:T(8,128)} %bitcast.124) | data formatting | bytes 2097152 | tf_op jit(solution)/shard_map/jit(_take)/gather | solution.py:57
  311.5 61.2 %all-to-all-done = f32[128,1,4,2,1024]{4,3,2,1,0:T(2,128)} async-done(((f32[128,1,4,2,1024]{4,3,2,1,0:T(2,128)}), f32[128,1,4,2,1024]{4,3,2,1,0:T(2,128)}, u32[]{:S(2)}, u32[]{:S(2)}) %all-to-all-start) | async-done | bytes 4194336 | tf_op jit(solution)/shard_map/all_to_all | solution.py:107
  372.7 4.8 %gather_fusion.2 = f32[32,4,2,1024]{3,2,1,0:T(2,128)} fusion(f32[128,4,2,1024]{3,2,1,0:T(2,128)} %bitcast.30, s32[1024]{0:T(1024)S(1)} %pad_clamp_fusion), kind=kCustom, calls=%fused_computation.4 | custom fusion | bytes 2097280 | tf_op jit(solution)/shard_map/jit(_take)/gather | solution.py:109
  377.5 1.7 bitcast_select_fusion.2
  379.2 1.1 pad_slice_fusion.7
  381.1 6.9 %broadcast_select_fusion.1 = f32[16,128,2,1024]{3,1,2,0:T(8,128)} fusion(f32[128,2,1024]{2,0,1:T(8,128)S(1)} %copy.100, f32[128,2,1024]{2,0,1:T(8,128)S(1)} %copy.99, pred[16,128]{1,0:T(8,128)(4,1)S(1)} %get-tuple-element.29), kind=kLoop, calls=%fused_computation.24 | loop fusion | flops 4194304 | bytes 18876416 | tf_op jit(solution)/shard_map/while/body/eval_jaxpr/vmap(jit(_where))/select_n | solution.py:39
  388.0 14.8 %fusion = f32[16,128,2,1024]{3,1,2,0:T(8,128)S(1)} fusion(f32[16,128,2,1024]{3,1,2,0:T(8,128)} %broadcast_select_fusion.1, pred[16,128]{1,0:T(8,128)(4,1)S(1)} %get-tuple-element.30), kind=kLoop, calls=%fused_computation.13 | loop fusion | flops 4194304 | bytes 33556480 | tf_op jit(solution)/shard_map/while/body/eval_jaxpr/vmap(jit(_where))/select_n | solution.py:39
  402.8 8.4 %fusion.1 = f32[16,128,2,1024]{3,1,2,0:T(8,128)} fusion(f32[16,128,2,1024]{3,1,2,0:T(8,128)S(1)} %fusion, pred[16,128]{1,0:T(8,128)(4,1)S(1)} %get-tuple-element.24), kind=kLoop, calls=%fused_computation.14 | loop fusion | flops 4194304 | bytes 33556480 | tf_op jit(solution)/shard_map/while/body/eval_jaxpr/vmap(jit(_where))/select_n | solution.py:39
  411.2 14.8 %fusion.2 = f32[16,128,2,1024]{3,1,2,0:T(8,128)S(1)} fusion(f32[16,128,2,1024]{3,1,2,0:T(8,128)} %fusion.1, pred[16,128]{1,0:T(8,128)(4,1)S(1)} %get-tuple-element.25), kind=kLoop, calls=%fused_computation.15 | loop fusion | flops 4194304 | bytes 33556480 | tf_op jit(solution)/shard_map/while/body/eval_jaxpr/vmap(jit(_where))/select_n | solution.py:39
  426.1 8.4 %fusion.3 = f32[16,128,2,1024]{3,1,2,0:T(8,128)} fusion(f32[16,128,2,1024]{3,1,2,0:T(8,128)S(1)} %fusion.2, pred[16,128]{1,0:T(8,128)(4,1)S(1)} %get-tuple-element.26), kind=kLoop, calls=%fused_computation.16 | loop fusion | flops 4194304 | bytes 33556480 | tf_op jit(solution)/shard_map/while/body/eval_jaxpr/vmap(jit(_where))/select_n | solution.py:39
  434.5 19.0 %fusion.4 = f32[16,128,2,1024]{3,1,2,0:T(8,128)} fusion(f32[16,128,2,1024]{3,1,2,0:T(8,128)} %fusion.3, pred[16,128]{1,0:T(8,128)(4,1)S(1)} %get-tuple-element.27), kind=kLoop, calls=%fused_computation.17 | loop fusion | flops 4194304 | bytes 33556480 | tf_op jit(solution)/shard_map/while/body/eval_jaxpr/vmap(jit(_where))/select_n | solution.py:39
  453.4 14.9 %fusion.5 = f32[16,128,2,1024]{3,1,2,0:T(8,128)S(1)} fusion(f32[16,128,2,1024]{3,1,2,0:T(8,128)} %fusion.4, pred[16,128]{1,0:T(8,128)(4,1)S(1)} %get-tuple-element.28), kind=kLoop, calls=%fused_computation.18 | loop fusion | flops 4194304 | bytes 33556480 | tf_op jit(solution)/shard_map/while/body/eval_jaxpr/vmap(jit(_where))/select_n | solution.py:39
  468.3 3.7 fusion.8
  472.2 1.0 fusion.14
  473.3 2.3 convolution_add_fusion
  475.5 0.7 reshape.541
  (58 shorter events, 3.7 us)
Async XLA Ops:
  0.0 101.6 %copy-start = (bf16[16,4,6,2,1024]{4,3,2,1,0:T(2,128)(2,1)S(1)}, bf16[16,4,6,2,1024]{4,3,2,1,0:T(2,128)(2,1)}, u32[]{:S(2)}) copy-start(bf16[16,4,6,2,1024]{4,3,2,1,0:T(2,128)(2,1)} %param.9) | copy-start | bytes 4718596
  145.3 44.6 %copy-start.5 = (s32[1,32]{1,0:T(1,128)S(1)}, s32[1,32]{1,0:T(1,128)}, u32[]{:S(2)}) copy-start(s32[1,32]{1,0:T(1,128)} %param.10) | copy-start | bytes 388
  145.3 45.7 %copy-start.2 = (f32[1,16,128]{2,1,0:T(8,128)S(1)}, f32[1,16,128]{2,1,0:T(8,128)}, u32[]{:S(2)}) copy-start(f32[1,16,128]{2,1,0:T(8,128)} %param.15) | copy-start | bytes 24580
  179.3 193.4 %all-to-all-start = ((f32[128,1,4,2,1024]{4,3,2,1,0:T(2,128)}), f32[128,1,4,2,1024]{4,3,2,1,0:T(2,128)}, u32[]{:S(2)}, u32[]{:S(2)}) async-start(f32[128,1,4,2,1024]{4,3,2,1,0:T(2,128)} %bitcast.123), calls=%async_computation | async-start | bytes 8388608 | tf_op jit(solution)/shard_map/all_to_all | solution.py:107
  191.1 120.3 %copy-start.4 = (f32[1,16,128]{2,1,0:T(8,128)S(1)}, f32[1,16,128]{2,1,0:T(8,128)}, u32[]{:S(2)}) copy-start(f32[1,16,128]{2,1,0:T(8,128)} %param.13) | copy-start | bytes 24580
  191.1 120.4 %copy-start.3 = (s32[1,16,128]{2,1,0:T(8,128)S(1)}, s32[1,16,128]{2,1,0:T(8,128)}, u32[]{:S(2)}) copy-start(s32[1,16,128]{2,1,0:T(8,128)} %param.12) | copy-start | bytes 24580
  453.4 22.8 %copy-start.1 = (bf16[16,4,6,2,1024]{4,3,2,1,0:T(2,128)(2,1)S(1)}, bf16[16,4,6,2,1024]{4,3,2,1,0:T(2,128)(2,1)}, u32[]{:S(2)}) copy-start(bf16[16,4,6,2,1024]{4,3,2,1,0:T(2,128)(2,1)} %param.9) | copy-start | bytes 4718596
where the time goes:
time: 480 us; the launch traced here: 476 us
  local copies, waits for them, and re-layouts  162 us (34%)
  other arithmetic  109 us (23%)
  blocking collectives  99.2 us (21%)
  waiting for transfers between devices  61.2 us (13%)
  matrix products  33.2 us (7%)
  starting transfers between devices  10.4 us (2%)
    all_gather x6, blocking collectives, stacked_from(): blocks = lax.all_gather(blocks, axes[k], axis=0, tiled=True)  99.2 us
    select_n x7, other arithmetic, lag_traces(): shifted_all = jnp.where(bit_set[:, None, None], shifted, shifted_all)  87.2 us
    all_to_all x1, waiting for transfers between devices, local(): lax.all_to_all(outgoing, PTS, split_axis=0, concat_axis=0, tiled=True)  61.2 us
    gather x2, local copies, waits for them, and re-layouts, convolve_rate(): jnp.take(slip_rate, jnp.clip(offset + taps, 0, taps - 1), axis=-1)  60.5 us
    gather x2, local copies, waits for them, and re-layouts, convolve_rate(): jnp.take(slip_rate, jnp.clip(offset, 0, taps - 1), axis=-1)  59.6 us
    dot_general x1, matrix products, local(): jnp.einsum('wcpsgt,wcs->wcpgt', picked, slot_mech, precision=lax.Precisio...  29.9 us
    gather x1, local copies, waits for them, and re-layouts, local(): picked = jnp.take(green_tensors, slot_block.reshape(-1), axis=0)  27.6 us
    select_n x2, other arithmetic, local(): picked = jnp.take(green_tensors, slot_block.reshape(-1), axis=0)  15.3 us
  transfers between devices with their start and end apart: 1, of which 1 were waited for; matrix products, arithmetic and copies ran while one was open for 25% of the time, Pallas kernels for 0%

commit v1 on v0

v1 whole, which is shorter than its diff:
```python
import functools

import jax
import jax.numpy as jnp
import numpy as np
from jax import lax
from jax.experimental import pallas as pl
from jax.experimental.pallas import tpu as pltpu
from jax.sharding import PartitionSpec as P

MESH = pl.DeviceIdType.MESH
HIGHEST = lax.Precision.HIGHEST
SITE_PTS = ("site", "pts")
PLANE = 8
LIMIT = 6.0
TOP = 32767.0
CHUNK = 4
BLOCKS = 16
VMEM_LIMIT = 60 * 1024 * 1024


def mate(j, e):
    for bit in (1, 2, 4):
        if e & bit:
            j = j + bit * (1 - 2 * ((j // bit) % 2))
    return j


def partner(index):
    return {"pts": index}


def train_of(planes):
    half = planes // 2
    dz = np.arange(planes * PLANE) // PLANE
    e = np.arange(planes * PLANE) % PLANE
    up = ((dz >= 1) & (dz < half)) | ((dz == half) & (e < PLANE // 2))
    down = (dz > half) | ((dz == half) & (e >= PLANE // 2))
    distance = np.where(up, dz, np.where(down, planes - dz, 0))
    return distance, up.astype(np.int32) - down.astype(np.int32), e


def before_table(planes):
    distance, way, e = train_of(planes)
    same = (way[:, None] == way[None, :]) & (way[:, None] != 0)
    ahead = (distance[:, None] > distance[None, :]) | (
        (distance[:, None] == distance[None, :]) & (e[:, None] < e[None, :])
    )
    return (same & ahead).astype(np.float32)


def reach_tables(planes, caps):
    distance, way, e = train_of(planes)
    half = planes // 2
    size = planes * PLANE
    reach = np.zeros((size, size), np.float32)
    limit = np.full((4 * planes, size), 1e6, np.float32)
    for chip in range(4):
        turned = np.arange(size) ^ (2 * chip)
        for s in range(1, half + 1):
            for w, sign in enumerate((1, -1)):
                column = chip * planes + w * half + s - 1
                reach[:, column] = ((way == sign) & (distance >= s))[turned]
                limit[chip * planes : (chip + 1) * planes, column] = caps[s - 1]
    return reach, limit


def most_packets(planes):
    half = planes // 2
    return tuple(2 * (PLANE * (half - s) + PLANE // 2) for s in range(1, half + 1))


def exchange_kernel(
    planes, list_ref, count_ref, moment_ref, before_ref, reach_ref, limit_ref, green_ref,
    tab_ref, block_ref, place_ref, over_ref, other_ref,
    row_ref, rows_ref, send_a, recv_a, send_b, recv_b, send_g, recv_g,
):
    me = lax.axis_index("pts")
    z, j = me // PLANE, me % PLANE
    size = planes * PLANE
    listed = list_ref.shape[1]
    strains = moment_ref.shape[1]

    barrier = pltpu.get_barrier_semaphore()
    for e in range(1, PLANE):
        pl.semaphore_signal(
            barrier, inc=1, device_id=partner(z * PLANE + mate(j, e)), device_id_type=MESH
        )
    for d in range(1, planes):
        pl.semaphore_signal(
            barrier, inc=1, device_id=partner(((z + d) % planes) * PLANE + j), device_id_type=MESH
        )
    entry = lax.broadcasted_iota(jnp.int32, (1, listed), 1)
    names = jnp.where(entry < count_ref[0], list_ref[...], -1).astype(jnp.float32)
    row_ref[...] = jnp.zeros_like(row_ref)
    row_ref[0, :, pl.ds(0, listed)] = names
    row_ref[0, :, pl.ds(listed + 1, strains)] = moment_ref[...]
    rows_ref[pl.ds(0, 1)] = row_ref[...]
    pl.semaphore_wait(barrier, PLANE - 1 + planes - 1)

    copies = []
    for e in range(1, PLANE):
        copies.append(
            pltpu.make_async_remote_copy(
                src_ref=row_ref,
                dst_ref=rows_ref.at[pl.ds(e, 1)],
                send_sem=send_a.at[e],
                recv_sem=recv_a.at[e],
                device_id=partner(z * PLANE + mate(j, e)),
                device_id_type=MESH,
            )
        )
    for copy in copies:
        copy.start()
    green = pltpu.make_async_remote_copy(
        src_ref=green_ref,
        dst_ref=other_ref,
        send_sem=send_g,
        recv_sem=recv_g,
        device_id=partner(z * PLANE + mate(j, 1)),
        device_id_type=MESH,
    )
    green.start()
    for copy in copies:
        copy.wait()
    copies = []
    for d in range(1, planes):
        copies.append(
            pltpu.make_async_remote_copy(
                src_ref=rows_ref.at[pl.ds(0, PLANE)],
                dst_ref=rows_ref.at[pl.ds((planes - d) * PLANE, PLANE)],
                send_sem=send_b.at[d],
                recv_sem=recv_b.at[d],
                device_id=partner(((z + d) % planes) * PLANE + j),
                device_id_type=MESH,
            )
        )
    for copy in copies:
        copy.start()
    for copy in copies:
        copy.wait()

    turned = rows_ref[...].reshape(size, 128).T
    named = turned[:listed]
    holder = jnp.floor(named * (1.0 / BLOCKS))
    source = lax.broadcasted_iota(jnp.int32, (size, size), 0)
    lane = lax.broadcasted_iota(jnp.int32, (size, size), 1)
    at = (z + planes - (source & (planes - 1))) & (planes - 1)
    source_id = (at * PLANE + (j ^ (source // planes))).astype(jnp.float32)
    active = jnp.zeros((size, size), jnp.float32)
    for k in range(listed):
        active = active + jnp.where(holder[k : k + 1, :] == source_id, 1.0, 0.0)
    view = pltpu.roll(active, 0, 1, stride=PLANE, stride_axis=0)
    chips = jnp.concatenate(
        [
            view[2 * g * planes : (2 * g + 1) * planes] + view[(2 * g + 1) * planes : (2 * g + 2) * planes]
            for g in range(4)
        ],
        axis=0,
    ).astype(jnp.bfloat16)
    counts = jnp.dot(chips, reach_ref[...], preferred_element_type=jnp.float32)
    excess = jnp.max(counts - limit_ref[...], axis=0, keepdims=True)
    excess = jnp.max(excess, axis=1, keepdims=True)
    over_ref[...] = jnp.broadcast_to(jnp.where(excess > 0.5, 1, 0), (8, 128)).astype(jnp.int32)

    first = jnp.dot(chips[:planes], before_ref[...], preferred_element_type=jnp.float32)
    second = first + view[:planes]
    diagonal = (lane[:planes] // PLANE) == source[:planes]
    part = lax.broadcasted_iota(jnp.int32, (8, size), 0)
    place = jnp.where(
        part == 0,
        jnp.sum(jnp.where(diagonal, first, 0.0), axis=0, keepdims=True),
        jnp.sum(jnp.where(diagonal, second, 0.0), axis=0, keepdims=True),
    )
    place_ref[...] = place.astype(jnp.int32)

    moment = turned[32:40]
    bound = LIMIT * jnp.sum(
        jnp.where((part >= 1) & (part <= strains), jnp.abs(moment), 0.0), axis=0, keepdims=True
    )
    gain = 1.0 / jnp.maximum(bound, 1e-30)
    moment = jnp.where(part == 7, gain, moment)
    side = lane[:1]
    way = jnp.where(side < PLANE, 0, jnp.where(side < (planes // 2) * PLANE + PLANE // 2, 1, -1))
    mine = way == 1 - 2 * (j % 2)
    slot = source.astype(jnp.float32)

    def info(owner, shift):
        owner = owner.astype(jnp.float32)
        block = jnp.where(holder == owner, named - (BLOCKS * owner - shift), 0.0)
        return jnp.where(part == 0, jnp.sum(block, axis=0, keepdims=True), moment)

    def table(which, held, position):
        chosen = (held > 0.5) & mine & (position == slot)
        return lax.dot_general(
            which,
            jnp.where(chosen, 1.0, 0.0),
            (((1,), (1,)), ((), ())),
            precision=HIGHEST,
            preferred_element_type=jnp.float32,
        )

    own = info(me, 0.0)
    both = table(own, view[:1], first[:1]) + table(
        info(me + 1 - 2 * (j % 2), float(BLOCKS)), view[planes : planes + 1], second[:1]
    )
    tab_ref[:, :size] = both
    tab_ref[:, size:] = own
    block_ref[:, :size] = both.astype(jnp.int32)
    block_ref[:, size:] = own.astype(jnp.int32)
    green.wait()


def exchange(planes, caps, lists, count, moment, green):
    size = planes * PLANE
    before = before_table(planes)
    reach, limit = reach_tables(planes, caps)
    vmem = pl.BlockSpec(memory_space=pltpu.VMEM)
    smem = pl.BlockSpec(memory_space=pltpu.SMEM)
    hbm = pl.BlockSpec(memory_space=pl.ANY)
    return pl.pallas_call(
        functools.partial(exchange_kernel, planes),
        out_shape=(
            jax.ShapeDtypeStruct((8, 2 * size), jnp.float32),
            jax.ShapeDtypeStruct((8, 2 * size), jnp.int32),
            jax.ShapeDtypeStruct((8, size), jnp.int32),
            jax.ShapeDtypeStruct((8, 128), jnp.int32),
            jax.ShapeDtypeStruct(green.shape, green.dtype),
        ),
        in_specs=[vmem, smem, vmem, vmem, vmem, vmem, hbm],
        out_specs=(vmem, vmem, vmem, vmem, hbm),
        scratch_shapes=[
            pltpu.VMEM((1, 1, 128), jnp.float32),
            pltpu.VMEM((size, 1, 128), jnp.float32),
            pltpu.SemaphoreType.DMA((PLANE,)),
            pltpu.SemaphoreType.DMA((PLANE,)),
            pltpu.SemaphoreType.DMA((planes,)),
            pltpu.SemaphoreType.DMA((planes,)),
            pltpu.SemaphoreType.DMA,
            pltpu.SemaphoreType.DMA,
        ],
        compiler_params=pltpu.CompilerParams(collective_id=0, has_side_effects=True),
        name="exchange",
    )(
        lists, count, moment, jnp.asarray(before, jnp.bfloat16), jnp.asarray(reach, jnp.bfloat16),
        jnp.asarray(limit), green,
    )


def spans(count):
    return [(first, min(first + CHUNK, count)) for first in range(0, count, CHUNK)]


def carry_kernel(planes, caps, place_ref, block_ref, tab_ref, mine_ref, other_ref, out_ref, *scratch):
    half = planes // 2
    green, own, staged, near = scratch[:4]
    moved = scratch[4 : 4 + half]
    load, send_z, recv_z, send_x, recv_x, send_n, recv_n = scratch[4 + half :]
    me = lax.axis_index("pts")
    z, j = me // PLANE, me % PLANE
    w = j % 2
    size = planes * PLANE

    loads = [
        pltpu.make_async_copy(mine_ref, green.at[pl.ds(0, BLOCKS)], load.at[0]),
        pltpu.make_async_copy(other_ref, green.at[pl.ds(BLOCKS, BLOCKS)], load.at[1]),
    ]
    for copy in loads:
        copy.start()
    barrier = pltpu.get_barrier_semaphore()
    for e in range(1, PLANE):
        pl.semaphore_signal(
            barrier, inc=1, device_id=partner(z * PLANE + mate(j, e)), device_id_type=MESH
        )
    for way in (1, planes - 1):
        pl.semaphore_signal(
            barrier, inc=1, device_id=partner(((z + way) % planes) * PLANE + j), device_id_type=MESH
        )
    for copy in loads:
        copy.wait()
    pl.semaphore_wait(barrier, PLANE - 1 + 2)

    def trace(entry, write):
        block = jnp.clip(block_ref[0, entry], 0, 2 * BLOCKS - 1)
        moment = [tab_ref[1 + s, entry] for s in range(6)]
        gain = tab_ref[7, entry]
        for p in range(4):
            total = moment[0] * green[block, p, 0].astype(jnp.float32)
            for s in range(1, 6):
                total = total + moment[s] * green[block, p, s].astype(jnp.float32)
            root = lax.rsqrt(lax.rsqrt(jnp.abs(total) * gain))
            level = jnp.minimum(root * TOP, TOP)
            code = jnp.round(jnp.where(total < 0.0, -level, level)).astype(jnp.int32)
            write(p, code.astype(jnp.int16))

    def hop(s, c):
        first, last = spans(caps[s])[c]
        source = own if s == 0 else moved[s - 1]
        return pltpu.make_async_remote_copy(
            src_ref=source.at[pl.ds(first, last - first)],
            dst_ref=moved[s].at[pl.ds(first, last - first)],
            send_sem=send_z.at[s, c],
            recv_sem=recv_z.at[s, c],
            device_id=partner(((z + 1 + w * (planes - 2)) % planes) * PLANE + j),
            device_id_type=MESH,
        )

    def offset(s):
        return (s + 1) + w * (planes - 2 * (s + 1))

    def spread(s, e):
        return pltpu.make_async_remote_copy(
            src_ref=staged.at[s, e],
            dst_ref=out_ref.at[offset(s), pl.ds(e - e % 2, 2)],
            send_sem=send_x.at[s, e],
            recv_sem=recv_x.at[offset(s), e // 2],
            device_id=partner(z * PLANE + mate(j, e)),
            device_id_type=MESH,
        )

    def visit(e):
        return pltpu.make_async_remote_copy(
            src_ref=near.at[e],
            dst_ref=out_ref.at[0, e],
            send_sem=send_n.at[e],
            recv_sem=recv_n.at[e],
            device_id=partner(z * PLANE + mate(j, e)),
            device_id_type=MESH,
        )

    for c, (first, last) in enumerate(spans(caps[0])):

        def fill(i, carry):
            def write(p, code):
                own[i, pl.ds(16 * p, 16), :] = code

            trace(i, write)
            return carry

        lax.fori_loop(first, last, fill, 0)
        hop(0, c).start()

    def write_own(p, code):
        out_ref[0, 0, pl.ds(16 * p, 16), :] = code

    trace(size, write_own)

    def fill_near(e, carry):
        def write(p, code):
            near[e, pl.ds(16 * p, 16), :] = code

        trace(size + e, write)
        return carry

    lax.fori_loop(1, PLANE, fill_near, 0)
    for e in range(1, PLANE):
        visit(e).start()

    def deliver(s, mates):
        q = offset(s)
        for e in mates:
            for r in range(2):
                at = jnp.clip(place_ref[r, q * PLANE + e], 0, caps[s] - 1)
                packet = moved[s][at]
                if e == 0:
                    out_ref[q, r] = packet
                else:
                    staged[s, e, (e + r) % 2] = packet
        for e in mates:
            if e:
                spread(s, e).start()

    low, high = range(PLANE // 2), range(PLANE // 2, PLANE)
    for s in range(half):
        for c, (first, last) in enumerate(spans(caps[s])):
            hop(s, c).wait_recv()
            if s + 1 < half and first < caps[s + 1]:
                hop(s + 1, c).start()
        if s + 1 < half:
            deliver(s, range(PLANE))
        else:

            @pl.when(w == 0)
            def _():
                deliver(half - 1, low)

            @pl.when(w == 1)
            def _():
                deliver(half - 1, high)

    for s in range(half):
        for c in range(len(spans(caps[s]))):
            hop(s, c).wait_send()
    for e in range(1, PLANE):
        visit(e).wait()
        for s in range(half - 1):
            spread(s, e).wait_send()

    @pl.when(w == 0)
    def _():
        for e in low:
            if e:
                spread(half - 1, e).wait_send()

    @pl.when(w == 1)
    def _():
        for e in high:
            spread(half - 1, e).wait_send()

    def arrival(q, chip):
        return pltpu.make_async_remote_copy(
            src_ref=staged.at[0, 1],
            dst_ref=out_ref.at[q, pl.ds(2 * chip, 2)],
            send_sem=send_x.at[0, 1],
            recv_sem=recv_x.at[q, chip],
            device_id=partner(z * PLANE + mate(j, 1)),
            device_id_type=MESH,
        )

    for q in range(1, planes):
        for chip in range(1, 4):
            arrival(q, chip).wait_recv()

    @pl.when(w == 1)
    def _():
        for q in range(1, half + 1):
            arrival(q, 0).wait_recv()

    @pl.when(w == 0)
    def _():
        for q in range(half + 1, planes):
            arrival(q, 0).wait_recv()


def carry(planes, caps, number, place, block, tab, mine, other):
    half = planes // 2
    chunks = len(spans(caps[0]))
    smem = pl.BlockSpec(memory_space=pltpu.SMEM)
    hbm = pl.BlockSpec(memory_space=pl.ANY)
    packet = (64, 128)
    return pl.pallas_call(
        functools.partial(carry_kernel, planes, caps),
        out_shape=jax.ShapeDtypeStruct((planes, PLANE, *packet), jnp.int16),
        in_specs=[smem, smem, smem, hbm, hbm],
        out_specs=pl.BlockSpec(memory_space=pltpu.VMEM),
        scratch_shapes=[
            pltpu.VMEM((2 * mine.shape[0], *mine.shape[1:]), mine.dtype),
            pltpu.VMEM((caps[0], *packet), jnp.int16),
            pltpu.VMEM((half, PLANE, 2, *packet), jnp.int16),
            pltpu.VMEM((PLANE, *packet), jnp.int16),
            *[pltpu.VMEM((caps[s], *packet), jnp.int16) for s in range(half)],
            pltpu.SemaphoreType.DMA((2,)),
            pltpu.SemaphoreType.DMA((half, chunks)),
            pltpu.SemaphoreType.DMA((half, chunks)),
            pltpu.SemaphoreType.DMA((half, PLANE)),
            pltpu.SemaphoreType.DMA((planes, 4)),
            pltpu.SemaphoreType.DMA((PLANE,)),
            pltpu.SemaphoreType.DMA((PLANE,)),
        ],
        compiler_params=pltpu.CompilerParams(
            collective_id=number, has_side_effects=True, vmem_limit_bytes=VMEM_LIMIT
        ),
        name="carry",
    )(place, block, tab, mine, other)


def halves(value):
    coarse = value.astype(jnp.bfloat16)
    return coarse, (value - coarse.astype(jnp.float32)).astype(jnp.bfloat16)


def motion_kernel(
    planes, list_ref, count_ref, onset_ref, slip_ref, moment_ref, packet_ref, rate_ref, out_ref,
    wide, motion,
):
    me = lax.axis_index("pts")
    z, j = me // PLANE, me % PLANE
    variations = out_ref.shape[0]
    bound = jnp.abs(moment_ref[0, 0])
    for s in range(1, 6):
        bound = bound + jnp.abs(moment_ref[0, s])
    unit = bound * (LIMIT / TOP**4)
    lane = lax.broadcasted_iota(jnp.int32, (16, 128), 1)
    motion[...] = jnp.zeros_like(motion)
    wide[...] = jnp.zeros_like(wide)

    def add_block(k, carry):
        holder = list_ref[0, k] // 16
        hz, hj = holder // PLANE, holder % PLANE
        q = (z - hz + planes) % planes
        e = j ^ hj
        for p in range(4):
            code = packet_ref[q, e, pl.ds(16 * p, 16), :].astype(jnp.int32).astype(jnp.float32)
            square = code * jnp.abs(code)
            wide[p, pl.ds(8, 16), :] = square * jnp.abs(square) * unit
        for v in range(variations):
            total = None
            for p in range(4):
                onset = onset_ref[v, k * 4 + p]
                whole = onset >> 7
                rest = onset & 127
                near = wide[p, pl.ds(8 - 2 * whole, 16), :]
                far = wide[p, pl.ds(6 - 2 * whole, 16), :]
                moved = pltpu.roll(jnp.where(lane < 128 - rest, near, far), rest, 1)
                term = slip_ref[v, k * 4 + p] * moved
                total = term if total is None else total + term
            motion[v, pl.ds(8, 16), :] += total
        return carry

    lax.fori_loop(0, count_ref[0], add_block, 0)

    row = lax.broadcasted_iota(jnp.int32, (128, 128), 0)
    column = lax.broadcasted_iota(jnp.int32, (128, 128), 1)
    for v in range(variations):
        rate = jnp.broadcast_to(rate_ref[pl.ds(v, 1), :], (128, 128))
        rate = pltpu.roll(rate, 0, 1, stride=1, stride_axis=0)
        taps = jnp.concatenate(
            [jnp.where(column >= row, rate, 0.0), jnp.where(column < row, rate, 0.0)], axis=0
        )
        signal = jnp.concatenate([motion[v, pl.ds(8, 16), :], motion[v, pl.ds(6, 16), :]], axis=1)
        coarse, fine = halves(signal)
        taps, rest = halves(taps)
        both = jnp.dot(
            jnp.concatenate([coarse, fine], axis=0), taps, preferred_element_type=jnp.float32
        )
        out_ref[v] = (
            both[:16] + both[16:] + jnp.dot(coarse, rest, preferred_element_type=jnp.float32)
        )


def synthesize(planes, block_list, count, onset, slip, moment, packets, rate):
    variations = onset.shape[0]
    smem = pl.BlockSpec(memory_space=pltpu.SMEM)
    vmem = pl.BlockSpec(memory_space=pltpu.VMEM)
    return pl.pallas_call(
        functools.partial(motion_kernel, planes),
        out_shape=jax.ShapeDtypeStruct((variations, 16, 128), jnp.float32),
        in_specs=[smem, smem, smem, smem, smem, vmem, vmem],
        out_specs=vmem,
        scratch_shapes=[
            pltpu.VMEM((4, 24, 128), jnp.float32),
            pltpu.VMEM((variations, 24, 128), jnp.float32),
        ],
        compiler_params=pltpu.CompilerParams(vmem_limit_bytes=VMEM_LIMIT),
        name="synthesize",
    )(block_list, count, onset, slip, moment, packets, rate)


CAPS = (37, 34, 30, 27, 23, 19, 14, 7)


def local(planes, green_tensors, block_lists, block_count, onset_steps, slip_amount, mechanism, slip_rate):
    held, points, strains, parts, length = green_tensors.shape
    green = green_tensors.reshape(held, points, strains, parts, length // 128, 128)
    green = green.transpose(0, 1, 2, 4, 3, 5).reshape(held, points, strains, -1, 128)
    tab, block, place, over, other = exchange(
        planes, CAPS, block_lists, block_count, mechanism, green
    )
    packets = lax.cond(
        over[0, 0] > 0,
        functools.partial(carry, planes, most_packets(planes), 1),
        functools.partial(carry, planes, CAPS, 2),
        place,
        block,
        tab,
        green,
        other,
    )
    seis = synthesize(
        planes, block_lists, block_count, onset_steps[0], slip_amount[0], mechanism, packets, slip_rate[0]
    )
    seis = seis.reshape(-1, length // 128, parts, 128).transpose(0, 2, 1, 3)
    return seis.reshape(1, -1, parts, length)


def solution(mesh):
    planes = mesh.shape["pts"] // PLANE
    placed = tuple(P(SITE_PTS, *[None] * n) for n in (4, 1, 0, 2, 2, 1, 2))
    return jax.shard_map(
        functools.partial(local, planes),
        mesh=mesh,
        in_specs=placed,
        out_specs=P(SITE_PTS, None, None, None),
        check_vma=False,
    )
```

time: 480 us -> 103 us (0.21)
  local copies, waits for them, and re-layouts: 162 us -> 1.19 us
  other arithmetic: 109 us -> 0 us
  blocking collectives: 99.2 us -> 0 us
  Pallas kernels: 0 us -> 98.7 us
  waiting for transfers between devices: 61.2 us -> 0 us
  matrix products: 33.2 us -> 0 us
  starting transfers between devices: 10.4 us -> 0 us
    gather x7 -> x0, local copies, waits for them, and re-layouts: 153 us -> none  [the longest x2 60.5 us: convolve_rate(): jnp.take(slip_rate, jnp.clip(offset + taps, 0, taps - 1), axis=-1)]
    select_n x13 -> x0, other arithmetic: 104 us -> none  [the longest x7 87.2 us: lag_traces(): shifted_all = jnp.where(bit_set[:, None, None], shifted, shifted_all)]
    all_gather x6 -> x0, blocking collectives: 99.2 us -> none  [stacked_from(): blocks = lax.all_gather(blocks, axes[k], axis=0, tiled=True)]
    pallas_call x0 -> x3, Pallas kernels: none -> 98.7 us  [the longest x1 49.5 us: carry(): pl.pallas_call(functools.partial(carry_kernel, planes, caps), out_shape=j...]
    all_to_all x1 -> x0, waiting for transfers between devices: 61.2 us -> none  [local(): lax.all_to_all(outgoing, PTS, split_axis=0, concat_axis=0, tiled=True)]
    dot_general x3 -> x0, matrix products: 33.2 us -> none  [the longest x1 29.9 us: local(): jnp.einsum('wcpsgt,wcs->wcpgt', picked, slot_mech, precision=lax.Precisio...]
    all_to_all x1 -> x0, starting transfers between devices: 10.4 us -> none  [local(): lax.all_to_all(outgoing, PTS, split_axis=0, concat_axis=0, tiled=True)]
  transfers between devices with their start and end apart: 1 -> 0, of which waited for: 1 -> 0; matrix products, arithmetic and copies ran while one was open for 25% -> 0% of each run, Pallas kernels for 0% -> 0%
where the time goes in v1:
time: 103 us; the launch traced here: 101 us
  Pallas kernels  98.7 us (96%)
  between operations  1.32 us (1%)
  local copies, waits for them, and re-layouts  1.19 us (1%)
    pallas_call x1, Pallas kernels, carry(): pl.pallas_call(functools.partial(carry_kernel, planes, caps), out_shape=j...  49.5 us
    pallas_call x1, Pallas kernels, exchange(): pl.pallas_call(functools.partial(exchange_kernel, planes), out_shape=(jax...  38.8 us
    pallas_call x1, Pallas kernels, synthesize(): pl.pallas_call(functools.partial(motion_kernel, planes), out_shape=jax.Sh...  10.5 us

profile of v1, /device:TPU:35, one launch (start us, length us, event | category | flops | bytes accessed | tf_op | source)
XLA Modules:
  0.0 101.3 jit_solution(239418539270189168)
XLA Ops:
  0.7 38.8 %exchange.1 = (f32[8,256]{1,0:T(8,128)S(1)}, s32[8,256]{1,0:T(8,128)S(1)}, s32[8,128]{1,0:T(8,128)S(1)}, s32[8,128]{1,0:T(8,128)}, bf16[16,4,6,16,128]{4,3,2,1,0:T(8,128)(2,1)}) custom-call(s32[1,32]{1,0:T(1,128)} %list_ref.3, s32[1]{0:T(128)S(6)} %copy.15.count_ref, f32[1,6]{1,0:T(1,128)} %moment_ref.3, bf16[128,128]{1,0:T(8,128)(2,1)} %constant.9.clone.before_ref, ...), custom_call_target="tpu_custom_call" | custom-call | tf_op jit(solution)/shard_map/exchange/pallas_call | solution.py:221
  39.5 1.2 %slice.3 = s32[1,1]{1,0:T(1,128)} slice(s32[8,128]{1,0:T(8,128)} %get-tuple-element.43), slice={[0:1], [0:1]} | slice | bytes 8 | tf_op jit(solution)/shard_map/slice | solution.py:560
  41.3 49.5 %conditional.1 = (s16[16,8,64,128]{3,2,1,0:T(8,128)(2,1)S(1)}) conditional(s32[]{:T(128)} %bitcast.5, (s32[8,128]{1,0:T(8,128)S(1)}, s32[8,256]{1,0:T(8,128)S(1)}, f32[8,256]{1,0:T(8,128)S(1)}, bf16[16,4,6,16,128]{4,3,2,1,0:T(8,128)(2,1)}, bf16[16,4,6,16,128]{4,3,2,1,0:T(8,128)(2,1)}) %tuple.14, (s32[8,128]{1,0:T(8,128)S(1)}, s32[8,256]{1,0:T(8,128)S(1)}, ...), branch_computations={%region_0.0_spmd, %region_1.0_spmd} | conditional | bytes 8 | solution.py:559
  41.3 49.5 %carry.2 = s16[16,8,64,128]{3,2,1,0:T(8,128)(2,1)S(1)} custom-call(s32[8,128]{1,0:T(8,128)S(1)} %get-tuple-element.28.place_ref, s32[8,256]{1,0:T(8,128)S(1)} %get-tuple-element.29.block_ref, f32[8,256]{1,0:T(8,128)S(1)} %get-tuple-element.30.tab_ref, bf16[16,4,6,16,128]{4,3,2,1,0:T(8,128)(2,1)} %get-tuple-element.31.mine_ref, ...), custom_call_target="tpu_custom_call" | custom-call | tf_op jit(solution)/shard_map/cond/branch_0_fun/carry/pallas_call | solution.py:441
  90.8 10.5 %synthesize.1 = f32[16,16,128]{2,1,0:T(8,128)} custom-call(s32[1,32]{1,0:T(1,128)} %list_ref.3, s32[1]{0:T(128)S(6)} %copy.15.count_ref, s32[16,128]{1,0:T(8,128)} %bitcast.17, f32[16,128]{1,0:T(8,128)} %bitcast.18, f32[1,6]{1,0:T(1,128)} %moment_ref.3, s16[16,8,64,128]{3,2,1,0:T(8,128)(2,1)S(1)} %get-tuple-element.48.packet_ref, f32[16,128]{1,0:T(8,128)} %bitcast.19), custom_call_target="tpu_custom_call" | custom-call | tf_op jit(solution)/shard_map/synthesize/pallas_call | solution.py:535

commit v2 on v1

--- a/solution.py
+++ b/solution.py
@@ -70,9 +70,24 @@
     return tuple(2 * (PLANE * (half - s) + PLANE // 2) for s in range(1, half + 1))
 
 
+def turn_blocks(value):
+    rows, size = value.shape
+    skewed = pltpu.roll(value, 0, 1, stride=8, stride_axis=0)
+    row = lax.broadcasted_iota(jnp.int32, value.shape, 0)
+    block = lax.broadcasted_iota(jnp.int32, value.shape, 1) // 8
+    turned = jnp.zeros_like(value)
+    for n in range(rows):
+        picked = jnp.where(block == ((row + n) & (rows - 1)), skewed, 0.0)
+        picked = jnp.sum(picked, axis=0, keepdims=True)
+        if n:
+            picked = pltpu.roll(picked, size - 8 * n, 1)
+        turned = jnp.where(row == n, picked, turned)
+    return turned
+
+
 def exchange_kernel(
-    planes, list_ref, count_ref, moment_ref, before_ref, reach_ref, limit_ref, green_ref,
-    tab_ref, block_ref, place_ref, over_ref, other_ref,
+    planes, list_ref, count_ref, moment_ref, onset_ref, slip_ref, before_ref, reach_ref, limit_ref, green_ref,
+    tab_ref, block_ref, place_ref, over_ref, start_ref, rest_ref, weight_ref, other_ref,
     row_ref, rows_ref, send_a, recv_a, send_b, recv_b, send_g, recv_g,
 ):
     me = lax.axis_index("pts")
@@ -137,6 +152,10 @@
         )
     for copy in copies:
         copy.start()
+    onset = turn_blocks(onset_ref[...].astype(jnp.float32)).astype(jnp.int32)
+    start_ref[...] = 8 - 2 * (onset >> 7)
+    rest_ref[...] = onset & 127
+    weight_ref[...] = turn_blocks(slip_ref[...])
     for copy in copies:
         copy.wait()
 
@@ -161,7 +180,7 @@
     counts = jnp.dot(chips, reach_ref[...], preferred_element_type=jnp.float32)
     excess = jnp.max(counts - limit_ref[...], axis=0, keepdims=True)
     excess = jnp.max(excess, axis=1, keepdims=True)
-    over_ref[...] = jnp.broadcast_to(jnp.where(excess > 0.5, 1, 0), (8, 128)).astype(jnp.int32)
+    over_ref[...] = jnp.where(excess > 0.5, 1, 0).astype(jnp.int32)
 
     first = jnp.dot(chips[:planes], before_ref[...], preferred_element_type=jnp.float32)
     second = first + view[:planes]
@@ -211,7 +230,7 @@
     green.wait()
 
 
-def exchange(planes, caps, lists, count, moment, green):
+def exchange(planes, caps, lists, count, moment, onset, slip, green):
     size = planes * PLANE
     before = before_table(planes)
     reach, limit = reach_tables(planes, caps)
@@ -224,11 +243,14 @@
             jax.ShapeDtypeStruct((8, 2 * size), jnp.float32),
             jax.ShapeDtypeStruct((8, 2 * size), jnp.int32),
             jax.ShapeDtypeStruct((8, size), jnp.int32),
-            jax.ShapeDtypeStruct((8, 128), jnp.int32),
+            jax.ShapeDtypeStruct((1, 1), jnp.int32),
+            jax.ShapeDtypeStruct(onset.shape, jnp.int32),
+            jax.ShapeDtypeStruct(onset.shape, jnp.int32),
+            jax.ShapeDtypeStruct(slip.shape, jnp.float32),
             jax.ShapeDtypeStruct(green.shape, green.dtype),
         ),
-        in_specs=[vmem, smem, vmem, vmem, vmem, vmem, hbm],
-        out_specs=(vmem, vmem, vmem, vmem, hbm),
+        in_specs=[vmem, smem, vmem, vmem, vmem, vmem, vmem, vmem, hbm],
+        out_specs=(vmem, vmem, vmem, vmem, vmem, vmem, vmem, hbm),
         scratch_shapes=[
             pltpu.VMEM((1, 1, 128), jnp.float32),
             pltpu.VMEM((size, 1, 128), jnp.float32),
@@ -242,9 +264,12 @@
         compiler_params=pltpu.CompilerParams(collective_id=0, has_side_effects=True),
         name="exchange",
     )(
-        lists, count, moment, jnp.asarray(before, jnp.bfloat16), jnp.asarray(reach, jnp.bfloat16),
+        lists, count, moment, onset, slip, jnp.asarray(before, jnp.bfloat16), jnp.asarray(reach, jnp.bfloat16),
         jnp.asarray(limit), green,
     )
+
+
+RELAYED = 6
 
 
 def spans(count):
@@ -253,9 +278,9 @@
 
 def carry_kernel(planes, caps, place_ref, block_ref, tab_ref, mine_ref, other_ref, out_ref, *scratch):
     half = planes // 2
-    green, own, staged, near = scratch[:4]
-    moved = scratch[4 : 4 + half]
-    load, send_z, recv_z, send_x, recv_x, send_n, recv_n = scratch[4 + half :]
+    green, own, staged, near, relay = scratch[:5]
+    moved = scratch[5 : 5 + half]
+    (load, send_z, recv_z, send_x, recv_x, send_n, recv_n, send_r, recv_r, send_f) = scratch[5 + half :]
     me = lax.axis_index("pts")
     z, j = me // PLANE, me % PLANE
     w = j % 2
@@ -318,6 +343,33 @@
             device_id_type=MESH,
         )
 
+    beside = (j // 2 + 1 + 2 * w) % 4
+
+    def hand(s):
+        return pltpu.make_async_remote_copy(
+            src_ref=staged.at[s, pl.ds(4, 2)],
+            dst_ref=relay.at[s],
+            send_sem=send_r.at[s],
+            recv_sem=recv_r.at[s],
+            device_id=partner(z * PLANE + beside * 2 + w),
+            device_id_type=MESH,
+        )
+
+    def onward(s, i):
+        return pltpu.make_async_remote_copy(
+            src_ref=relay.at[s, i],
+            dst_ref=out_ref.at[offset(s), pl.ds(4, 2)],
+            send_sem=send_f.at[s, i],
+            recv_sem=recv_x.at[offset(s), 2],
+            device_id=partner(z * PLANE + beside * 2 + w + i * (1 - 2 * w)),
+            device_id_type=MESH,
+        )
+
+    def pass_on(s):
+        hand(s).wait_recv()
+        for i in range(2):
+            onward(s, i).start()
+
     def visit(e):
         return pltpu.make_async_remote_copy(
             src_ref=near.at[e],
@@ -366,8 +418,10 @@
                     out_ref[q, r] = packet
                 else:
                     staged[s, e, (e + r) % 2] = packet
+        if s < RELAYED:
+            hand(s).start()
         for e in mates:
-            if e:
+            if e and not (s < RELAYED and e // 2 == 2):
                 spread(s, e).start()
 
     low, high = range(PLANE // 2), range(PLANE // 2, PLANE)
@@ -378,6 +432,8 @@
                 hop(s + 1, c).start()
         if s + 1 < half:
             deliver(s, range(PLANE))
+            if 0 < s <= RELAYED:
+                pass_on(s - 1)
         else:
 
             @pl.when(w == 0)
@@ -394,7 +450,12 @@
     for e in range(1, PLANE):
         visit(e).wait()
         for s in range(half - 1):
-            spread(s, e).wait_send()
+            if not (s < RELAYED and e // 2 == 2):
+                spread(s, e).wait_send()
+    for s in range(RELAYED):
+        hand(s).wait_send()
+        for i in range(2):
+            onward(s, i).wait_send()
 
     @pl.when(w == 0)
     def _():
@@ -448,6 +509,7 @@
             pltpu.VMEM((caps[0], *packet), jnp.int16),
             pltpu.VMEM((half, PLANE, 2, *packet), jnp.int16),
             pltpu.VMEM((PLANE, *packet), jnp.int16),
+            pltpu.VMEM((RELAYED, 2, 2, *packet), jnp.int16),
             *[pltpu.VMEM((caps[s], *packet), jnp.int16) for s in range(half)],
             pltpu.SemaphoreType.DMA((2,)),
             pltpu.SemaphoreType.DMA((half, chunks)),
@@ -456,6 +518,9 @@
             pltpu.SemaphoreType.DMA((planes, 4)),
             pltpu.SemaphoreType.DMA((PLANE,)),
             pltpu.SemaphoreType.DMA((PLANE,)),
+            pltpu.SemaphoreType.DMA((RELAYED,)),
+            pltpu.SemaphoreType.DMA((RELAYED,)),
+            pltpu.SemaphoreType.DMA((RELAYED, 2)),
         ],
         compiler_params=pltpu.CompilerParams(
             collective_id=number, has_side_effects=True, vmem_limit_bytes=VMEM_LIMIT
@@ -470,8 +535,8 @@
 
 
 def motion_kernel(
-    planes, list_ref, count_ref, onset_ref, slip_ref, moment_ref, packet_ref, rate_ref, out_ref,
-    wide, motion,
+    planes, list_ref, count_ref, start_ref, rest_ref, slip_ref, moment_ref, packet_ref, rate_ref, out_ref,
+    near, far, motion,
 ):
     me = lax.axis_index("pts")
     z, j = me // PLANE, me % PLANE
@@ -479,35 +544,39 @@
     bound = jnp.abs(moment_ref[0, 0])
     for s in range(1, 6):
         bound = bound + jnp.abs(moment_ref[0, s])
-    unit = bound * (LIMIT / TOP**4)
     lane = lax.broadcasted_iota(jnp.int32, (16, 128), 1)
     motion[...] = jnp.zeros_like(motion)
-    wide[...] = jnp.zeros_like(wide)
-
-    def add_block(k, carry):
-        holder = list_ref[0, k] // 16
-        hz, hj = holder // PLANE, holder % PLANE
-        q = (z - hz + planes) % planes
-        e = j ^ hj
-        for p in range(4):
-            code = packet_ref[q, e, pl.ds(16 * p, 16), :].astype(jnp.int32).astype(jnp.float32)
-            square = code * jnp.abs(code)
-            wide[p, pl.ds(8, 16), :] = square * jnp.abs(square) * unit
+    near[...] = jnp.zeros_like(near)
+    far[...] = jnp.zeros_like(far)
+    count = count_ref[0]
+
+    def add_blocks(pair, carry):
+        for n in range(2):
+            k = 2 * pair + n
+            holder = list_ref[0, k] // BLOCKS
+            q = (z - holder // PLANE + planes) % planes
+            e = j ^ (holder % PLANE)
+            unit = jnp.where(k < count, bound, 0.0) * (LIMIT / TOP**4)
+            for p in range(4):
+                code = packet_ref[q, e, pl.ds(16 * p, 16), :].astype(jnp.int32).astype(jnp.float32)
+                square = code * jnp.abs(code)
+                trace = square * jnp.abs(square) * unit
+                near[4 * n + p, pl.ds(8, 16), :] = trace
+                far[4 * n + p, pl.ds(10, 16), :] = trace
         for v in range(variations):
             total = None
-            for p in range(4):
-                onset = onset_ref[v, k * 4 + p]
-                whole = onset >> 7
-                rest = onset & 127
-                near = wide[p, pl.ds(8 - 2 * whole, 16), :]
-                far = wide[p, pl.ds(6 - 2 * whole, 16), :]
-                moved = pltpu.roll(jnp.where(lane < 128 - rest, near, far), rest, 1)
-                term = slip_ref[v, k * 4 + p] * moved
+            for i in range(8):
+                start = start_ref[pair, v * 8 + i]
+                rest = rest_ref[pair, v * 8 + i]
+                trace = jnp.where(
+                    lane + rest < 128, near[i, pl.ds(start, 16), :], far[i, pl.ds(start, 16), :]
+                )
+                term = slip_ref[pair, v * 8 + i] * pltpu.roll(trace, rest, 1)
                 total = term if total is None else total + term
             motion[v, pl.ds(8, 16), :] += total
         return carry
 
-    lax.fori_loop(0, count_ref[0], add_block, 0)
+    lax.fori_loop(0, (count + 1) // 2, add_blocks, 0)
 
     row = lax.broadcasted_iota(jnp.int32, (128, 128), 0)
     column = lax.broadcasted_iota(jnp.int32, (128, 128), 1)
@@ -528,33 +597,34 @@
         )
 
 
-def synthesize(planes, block_list, count, onset, slip, moment, packets, rate):
-    variations = onset.shape[0]
+def synthesize(planes, block_list, count, start, rest, slip, moment, packets, rate):
+    variations = slip.shape[0]
     smem = pl.BlockSpec(memory_space=pltpu.SMEM)
     vmem = pl.BlockSpec(memory_space=pltpu.VMEM)
     return pl.pallas_call(
         functools.partial(motion_kernel, planes),
         out_shape=jax.ShapeDtypeStruct((variations, 16, 128), jnp.float32),
-        in_specs=[smem, smem, smem, smem, smem, vmem, vmem],
+        in_specs=[smem, smem, smem, smem, smem, smem, vmem, vmem],
         out_specs=vmem,
         scratch_shapes=[
-            pltpu.VMEM((4, 24, 128), jnp.float32),
+            pltpu.VMEM((8, 24, 128), jnp.float32),
+            pltpu.VMEM((8, 32, 128), jnp.float32),
             pltpu.VMEM((variations, 24, 128), jnp.float32),
         ],
         compiler_params=pltpu.CompilerParams(vmem_limit_bytes=VMEM_LIMIT),
         name="synthesize",
-    )(block_list, count, onset, slip, moment, packets, rate)
-
-
-CAPS = (37, 34, 30, 27, 23, 19, 14, 7)
+    )(block_list, count, start, rest, slip, moment, packets, rate)
+
+
+CAPS = (36, 33, 29, 26, 22, 18, 13, 8)
 
 
 def local(planes, green_tensors, block_lists, block_count, onset_steps, slip_amount, mechanism, slip_rate):
     held, points, strains, parts, length = green_tensors.shape
     green = green_tensors.reshape(held, points, strains, parts, length // 128, 128)
     green = green.transpose(0, 1, 2, 4, 3, 5).reshape(held, points, strains, -1, 128)
-    tab, block, place, over, other = exchange(
-        planes, CAPS, block_lists, block_count, mechanism, green
+    tab, block, place, over, start, rest, weight, other = exchange(
+        planes, CAPS, block_lists, block_count, mechanism, onset_steps[0], slip_amount[0], green
     )
     packets = lax.cond(
         over[0, 0] > 0,
@@ -567,7 +637,7 @@
         other,
     )
     seis = synthesize(
-        planes, block_lists, block_count, onset_steps[0], slip_amount[0], mechanism, packets, slip_rate[0]
+        planes, block_lists, block_count, start, rest, weight, mechanism, packets, slip_rate[0]
     )
     seis = seis.reshape(-1, length // 128, parts, 128).transpose(0, 2, 1, 3)
     return seis.reshape(1, -1, parts, length)

time: 103 us -> 98.1 us (0.952)
  the two profiles are of different devices: /device:TPU:35 before, /device:TPU:43 now
where the time goes in v2:
time: 98.1 us; the launch traced here: 97.8 us
  Pallas kernels  96.3 us (98%)
  between operations  1.3 us (1%)
    pallas_call x1, Pallas kernels, carry(): pl.pallas_call(functools.partial(carry_kernel, planes, caps), out_shape=j...  49.1 us
    pallas_call x1, Pallas kernels, exchange(): pl.pallas_call(functools.partial(exchange_kernel, planes), out_shape=(jax...  38.9 us
    pallas_call x1, Pallas kernels, synthesize(): pl.pallas_call(functools.partial(motion_kernel, planes), out_shape=jax.Sh...  8.34 us

profile of v2, /device:TPU:43, one launch (start us, length us, event | category | flops | bytes accessed | tf_op | source)
XLA Modules:
  0.0 97.8 jit_solution(2747835913140240449)
XLA Ops:
  0.7 38.9 %exchange.1 = (f32[8,256]{1,0:T(8,128)S(1)}, s32[8,256]{1,0:T(8,128)S(1)}, s32[8,128]{1,0:T(8,128)S(1)}, s32[1,1]{1,0:T(1,128)}, s32[16,128]{1,0:T(8,128)}, /*in...) custom-call(s32[1,32]{1,0:T(1,128)} %list_ref.3, s32[1]{0:T(128)S(6)} %copy.15.count_ref, ...), custom_call_target="tpu_custom_call" | custom-call | tf_op jit(solution)/shard_map/exchange/pallas_call | solution.py:240
  40.2 49.3 %conditional.1 = (s16[16,8,64,128]{3,2,1,0:T(8,128)(2,1)S(1)}) conditional(s32[]{:T(128)} %bitcast.5, (s32[8,128]{1,0:T(8,128)S(1)}, s32[8,256]{1,0:T(8,128)S(1)}, f32[8,256]{1,0:T(8,128)S(1)}, bf16[16,4,6,16,128]{4,3,2,1,0:T(8,128)(2,1)}, bf16[16,4,6,16,128]{4,3,2,1,0:T(8,128)(2,1)}) %tuple.14, (s32[8,128]{1,0:T(8,128)S(1)}, s32[8,256]{1,0:T(8,128)S(1)}, ...), branch_computations={%region_0.0_spmd, %region_1.0_spmd} | conditional | bytes 8 | solution.py:629
  40.2 49.1 %carry.2 = s16[16,8,64,128]{3,2,1,0:T(8,128)(2,1)S(1)} custom-call(s32[8,128]{1,0:T(8,128)S(1)} %get-tuple-element.28.place_ref, s32[8,256]{1,0:T(8,128)S(1)} %get-tuple-element.29.block_ref, f32[8,256]{1,0:T(8,128)S(1)} %get-tuple-element.30.tab_ref, bf16[16,4,6,16,128]{4,3,2,1,0:T(8,128)(2,1)} %get-tuple-element.31.mine_ref, ...), custom_call_target="tpu_custom_call" | custom-call | tf_op jit(solution)/shard_map/cond/branch_0_fun/carry/pallas_call | solution.py:502
  89.5 8.3 %synthesize.1 = f32[16,16,128]{2,1,0:T(8,128)} custom-call(s32[1,32]{1,0:T(1,128)} %list_ref.3, s32[1]{0:T(128)S(6)} %copy.15.count_ref, s32[16,128]{1,0:T(8,128)} %get-tuple-element.46.start_ref, s32[16,128]{1,0:T(8,128)} %get-tuple-element.47.rest_ref, f32[16,128]{1,0:T(8,128)} %get-tuple-element.48.slip_ref, f32[1,6]{1,0:T(1,128)} %moment_ref.3, ...), custom_call_target="tpu_custom_call" | custom-call | tf_op jit(solution)/shard_map/synthesize/pallas_call | solution.py:604
